TPU v7x, 128 devices: a whole 4x4x4 slice. The times are simulated.
128 devices in a mesh: member: 64 (over y_hi, z, x, core), cell: 2 (over y_lo).
Axes of the slice: x: 4, y: 4 (y_hi: 2, y_lo: 2; y = y_hi * 2 + y_lo), z: 4, core: 2. Of those that a mesh axis runs over, the one named last changes fastest.
Arguments:
- background_physical: bfloat16 [64, 128, 192, 384], P('member', None, 'cell'), may hold values from -6 to 6
- probe_surface_harmonic: int32 [2048], replicated, may hold values from 0 to 49151
- reading_destination_part: int32 [2048], replicated, may hold values from 0 to 63
- observed_readings: float32 [2048], replicated, may hold values from -8 to 8
- reading_spread: float32 [2048], replicated, may hold values from 0.5 to 2
- harmonic_update_weight: float32 [192, 384], P('cell'), may hold values from 0.1 to 1
Outputs:
- increments: bfloat16 [64, 128, 192, 384], P('member', None, 'cell')
Inputs may be any that keep to these rules, and one draw needn't show every extreme that they name: `probe_surface_harmonic`: the index a * 384 + k of axial plane a and circumferential Fourier mode k. `reading_destination_part`: block b covers axial planes b * 2 to (b + 1) * 2 - 1.
All inputs are finite; a program needn't handle non-finite values.
Results may differ from a plain program's by a relative error of at most 0.0098.
Values may be sent and summed in bfloat16 or wider, within the bound.
A program may use at most 128 MiB of HBM per device.

v0:
```python
import jax
import jax.numpy as jnp
from jax import lax
from jax.sharding import PartitionSpec as P

NS_ITERS = 24


def copy_for_each(shard, axis):
    size = lax.axis_size(axis)
    return lax.all_to_all(
        jnp.broadcast_to(shard[None], (size, *shard.shape)), axis, 0, 0, tiled=True
    )


def taken_together(shard, axis):
    return copy_for_each(shard, axis).sum(axis=0)


def joined_along(pieces, dim):
    dims = list(pieces.shape[1:])
    dims[dim] *= pieces.shape[0]
    return jnp.moveaxis(pieces, 0, dim).reshape(dims)


def gather_directly(shard, axis, dim):
    return joined_along(copy_for_each(shard, axis), dim)


def split_up(shard, dim, size):
    before, after = (shard.shape[:dim], shard.shape[dim + 1 :])
    return jnp.moveaxis(shard.reshape(*before, size, -1, *after), dim, 0)


def edges_of(length, count):
    lap = length // count
    if lap >= 8:
        lap -= lap % 8
    return [lap * k for k in range(1, count)]


def several_exchanges(shard, axis, pieces, split_dim, concat_dim):
    blocks = split_up(shard, split_dim, lax.axis_size(axis))
    widest = max(range(1, max(2, blocks.ndim - 1)), key=lambda d: blocks.shape[d])
    gathered = []
    for piece in jnp.split(blocks, edges_of(blocks.shape[widest], pieces), axis=widest):
        if piece.size:
            gathered.append(lax.all_to_all(piece, axis, split_axis=0, concat_axis=0, tiled=True))
    return joined_along(jnp.concatenate(gathered, axis=widest), concat_dim)


def dft_basis(length):
    row_index = lax.broadcasted_iota(jnp.int32, (length, length), 0)
    col_index = lax.broadcasted_iota(jnp.int32, (length, length), 1)
    half_len = length // 2
    frequency = jnp.where(col_index <= half_len, col_index, col_index - half_len)
    product_mod = row_index * frequency % length
    phase_angle = 2.0 * jnp.pi * product_mod.astype(jnp.float32) / length
    basis_vals = jnp.where(col_index <= half_len, jnp.cos(phase_angle), jnp.sin(phase_angle))
    edge_cols = (col_index == 0) | (col_index == half_len)
    norm_factor = jnp.where(edge_cols, jnp.sqrt(1.0 / length), jnp.sqrt(2.0 / length))
    return (basis_vals * norm_factor).astype(jnp.bfloat16)


def mapping_operator(
    expected_readings,
    observed_readings,
    reading_spread,
    reading_destination_part,
    assigned_partition,
    member_number,
):
    observed_anomalies = lax.Precision.HIGHEST
    unit_diagonal = jnp.eye(member_number, dtype=jnp.float32)
    pred_mean = jnp.mean(expected_readings, axis=1)
    anomaly = expected_readings - pred_mean[:, None]
    selector = (reading_destination_part == assigned_partition).astype(jnp.float32) / reading_spread
    normalized_anomaly = anomaly * selector[:, None]
    innovation = (observed_readings - pred_mean) * selector
    inner_product_grid = (member_number - 1.0) * unit_diagonal + jnp.dot(
        normalized_anomaly.T, normalized_anomaly, precision=observed_anomalies
    )
    right_term = jnp.dot(normalized_anomaly.T, innovation, precision=observed_anomalies)
    norm_scale = jnp.sqrt(jnp.sum(inner_product_grid * inner_product_grid))

    def newton_iter(count, carry):
        iterate, inv_root = carry
        newton_step = 1.5 * unit_diagonal - 0.5 * jnp.dot(
            inv_root, iterate, precision=observed_anomalies
        )
        return (
            jnp.dot(iterate, newton_step, precision=observed_anomalies),
            jnp.dot(newton_step, inv_root, precision=observed_anomalies),
        )

    iterate, inv_root = lax.fori_loop(
        0, NS_ITERS, newton_iter, (inner_product_grid / norm_scale, unit_diagonal)
    )
    reciprocal_root = inv_root / jnp.sqrt(norm_scale)
    inv_gram = jnp.dot(reciprocal_root, reciprocal_root, precision=observed_anomalies)
    combination_factors = jnp.dot(inv_gram, right_term, precision=observed_anomalies)
    merged_product = combination_factors[:, None] + jnp.sqrt(member_number - 1.0) * reciprocal_root
    mean_removal = unit_diagonal - 1.0 / member_number
    complete_lookup = 1.0 / member_number + jnp.dot(
        mean_removal, merged_product, precision=observed_anomalies
    )
    return (complete_lookup - unit_diagonal).astype(jnp.bfloat16)


def spectral_conversion_pass(predicted_layouts, trigonometric_design):
    dimension_tuple = predicted_layouts.shape
    flat = jnp.dot(
        predicted_layouts.reshape(-1, dimension_tuple[-1]),
        trigonometric_design,
        preferred_element_type=jnp.float32,
    )
    return flat.astype(jnp.bfloat16).reshape(dimension_tuple)


def on_device(
    background_physical,
    probe_surface_harmonic,
    reading_destination_part,
    observed_readings,
    reading_spread,
    harmonic_update_weight,
):
    cells = lax.axis_size("cell")
    azimuth_perimeter = background_physical.shape[3]
    trigonometric_design = dft_basis(azimuth_perimeter)
    member_number = lax.axis_size("member")
    assigned_partition = lax.axis_index("member")
    top_cell = (lax.axis_index("cell") == cells - 1).astype(jnp.float32)
    spectral_coefficients = spectral_conversion_pass(background_physical, trigonometric_design)
    boundary_innovation = (
        spectral_coefficients[0, :, -1, :].astype(jnp.float32)
        - spectral_coefficients[0, :, -2, :].astype(jnp.float32)
    ) * top_cell
    own_preds = boundary_innovation.reshape(-1)[probe_surface_harmonic]
    own_preds = taken_together(own_preds, "cell")
    expected_readings = gather_directly(own_preds[:, None], "member", 1)
    blend_coefficients = mapping_operator(
        expected_readings,
        observed_readings,
        reading_spread,
        reading_destination_part,
        assigned_partition,
        member_number,
    )
    owned = several_exchanges(spectral_coefficients, "member", 2, 1, 0)
    changed = jnp.einsum(
        "ij,iabc->jabc", blend_coefficients, owned, preferred_element_type=jnp.float32
    )
    changed = (changed * harmonic_update_weight[None, None]).astype(jnp.bfloat16)
    returned = lax.all_to_all(changed, "member", split_axis=0, concat_axis=1, tiled=True)
    return spectral_conversion_pass(returned, trigonometric_design.T)


def solution(mesh):
    return jax.shard_map(
        on_device,
        mesh=mesh,
        in_specs=(P("member", None, "cell", None), P(), P(), P(), P(), P("cell", None)),
        out_specs=P("member", None, "cell", None),
        check_vma=False,
    )
```

profile of v0, /device:TPU:1, one launch (start us, length us, event | category | flops | bytes accessed | tf_op | source)
XLA Modules:
  0.0 361.9 jit_solution(4852711836953895450)
XLA Ops:
  0.0 17.0 %fusion.3 = bf16[12288,384]{0,1:T(8,128)(2,1)} fusion(bf16[12288,384]{1,0:T(8,128)(2,1)} %bitcast.81, f32[384]{0:T(512)S(1)} %fusion.40, s32[384]{0:T(512)S(1)} %iota_add_fusion, pred[384]{0:T(512)(128)(4,1)S(1)} %iota_compare_fusion.4), kind=kOutput, calls=%fused_computation.9 | convolution fusion | flops 3630514176 | bytes 18877824 | tf_op jit(solution)/shard_map/dot_general | solution.py:112
  17.0 12.7 %copy.38 = bf16[12288,384]{1,0:T(8,128)(2,1)} copy(bf16[12288,384]{0,1:T(8,128)(2,1)} %fusion.3) | data formatting | bytes 18874368 | tf_op jit(solution)/shard_map/convert_element_type | solution.py:117
  29.7 1.9 fusion.28
  31.6 11.8 %gather_fusion = f32[2048]{0:T(1024)S(1)} fusion(f32[49152]{0:T(1024)S(1)} %bitcast.78, s32[2048]{0:T(1024)S(1)} %fusion.38), kind=kCustom, calls=%fused_computation | custom fusion | bytes 24576 | tf_op jit(solution)/shard_map/gather | solution.py:139
  43.5 5.9 %all_to_all.30 = f32[2,1,2048]{2,1,0:T(1,128)S(1)} all-to-all(f32[2,1,2048]{2,1,0:T(1,128)S(1)} %broadcast_in_dim.29), channel_id=1, replica_groups=mesh['member'=64,'cell'=2] {'cell'}, dimensions={0} | all-to-all | bytes 32768 | tf_op jit(solution)/shard_map/all_to_all | solution.py:11
  49.4 1.0 broadcast_in_dim.30
  50.4 12.8 %all-to-all-start.1 = ((f32[64,2048,1]{1,2,0:T(1,128)}), f32[64,2048,1]{1,2,0:T(1,128)S(1)}, u32[]{:S(2)}, u32[]{:S(2)}) async-start(f32[64,2048,1]{1,2,0:T(1,128)} %broadcast_in_dim.30), calls=%async_computation.1 | async-start | bytes 1048576 | tf_op jit(solution)/shard_map/all_to_all | solution.py:11
  63.2 8.5 %slice_bitcast_fusion.1 = (bf16[64,1,2,48,384]{4,3,2,1,0:T(8,128)(2,1)}, bf16[64,1,2,48,384]{4,3,2,1,0:T(8,128)(2,1)}) fusion(bf16[64,1,2,96,384]{4,3,2,0,1:T(8,128)(2,1)} %bitcast.80), kind=kLoop, calls=%fused_computation.15 | loop fusion | bytes 18874368 | tf_op jit(solution)/shard_map/split | solution.py:46
  71.7 5.3 %all-to-all-done.1 = f32[64,2048,1]{1,2,0:T(1,128)S(1)} async-done(((f32[64,2048,1]{1,2,0:T(1,128)}), f32[64,2048,1]{1,2,0:T(1,128)S(1)}, u32[]{:S(2)}, u32[]{:S(2)}) %all-to-all-start.1) | async-done | bytes 524320 | tf_op jit(solution)/shard_map/all_to_all | solution.py:11
  77.0 5.4 %all-to-all-start.2 = ((bf16[64,1,2,48,384]{4,3,2,1,0:T(8,128)(2,1)}), bf16[64,1,2,48,384]{4,3,2,1,0:T(8,128)(2,1)}, u32[]{:S(2)}, u32[]{:S(2)}) async-start(bf16[64,1,2,48,384]{4,3,2,1,0:T(8,128)(2,1)} %get-tuple-element.59), calls=%async_computation.2 | async-start | bytes 9437184 | tf_op jit(solution)/shard_map/all_to_all | solution.py:48
  82.5 0.3 reduce_sum.28
  82.9 1.4 multiply_reduce_fusion
  85.1 57.4 %all-to-all-done.2 = bf16[64,1,2,48,384]{4,3,2,1,0:T(8,128)(2,1)} async-done(((bf16[64,1,2,48,384]{4,3,2,1,0:T(8,128)(2,1)}), bf16[64,1,2,48,384]{4,3,2,1,0:T(8,128)(2,1)}, u32[]{:S(2)}, u32[]{:S(2)}) %all-to-all-start.2) | async-done | bytes 4718624 | tf_op jit(solution)/shard_map/all_to_all | solution.py:48
  142.5 8.5 %all-to-all-start.3 = ((bf16[64,1,2,48,384]{4,3,2,1,0:T(8,128)(2,1)}), bf16[64,1,2,48,384]{4,3,2,1,0:T(8,128)(2,1)}, u32[]{:S(2)}, u32[]{:S(2)}) async-start(bf16[64,1,2,48,384]{4,3,2,1,0:T(8,128)(2,1)} %get-tuple-element.60), calls=%async_computation.3 | async-start | bytes 9437184 | tf_op jit(solution)/shard_map/all_to_all | solution.py:48
  150.9 15.5 %while.13 = (s32[]{:T(128)}, f32[64,64]{0,1:T(8,128)S(1)}, f32[64,64]{1,0:T(8,128)S(1)}, s32[]{:T(128)}) while((s32[]{:T(128)}, f32[64,64]{0,1:T(8,128)S(1)}, f32[64,64]{1,0:T(8,128)S(1)}, s32[]{:T(128)}) %tuple.30), condition=%wide.region_4.5_spmd.clone, body=%wide.region_3.4_spmd.clone.sunk | while | flops 9453570 | bytes 213045 | solution.py:96
  151.3 0.2 convolution_bitcast_fusion.4
  152.0 0.2 convolution_bitcast_fusion.4
  152.6 0.2 convolution_bitcast_fusion.4
  153.3 0.2 convolution_bitcast_fusion.4
  153.9 0.2 convolution_bitcast_fusion.4
  154.6 0.2 convolution_bitcast_fusion.4
  155.2 0.2 convolution_bitcast_fusion.4
  155.8 0.2 convolution_bitcast_fusion.4
  156.5 0.2 convolution_bitcast_fusion.4
  157.1 0.2 convolution_bitcast_fusion.4
  157.8 0.2 convolution_bitcast_fusion.4
  158.4 0.2 convolution_bitcast_fusion.4
  159.1 0.2 convolution_bitcast_fusion.4
  159.7 0.2 convolution_bitcast_fusion.4
  160.4 0.2 convolution_bitcast_fusion.4
  161.0 0.2 convolution_bitcast_fusion.4
  161.6 0.2 convolution_bitcast_fusion.4
  162.3 0.2 convolution_bitcast_fusion.4
  162.9 0.2 convolution_bitcast_fusion.4
  163.6 0.2 convolution_bitcast_fusion.4
  164.2 0.2 convolution_bitcast_fusion.4
  164.9 0.2 convolution_bitcast_fusion.4
  165.5 0.2 convolution_bitcast_fusion.4
  166.2 0.2 convolution_bitcast_fusion.4
  166.6 0.6 convolution_bitcast_fusion.2
  167.4 0.3 fusion.9
  167.7 6.3 %copy.45 = bf16[64,1,2,48,384]{4,0,3,2,1:T(8,128)(2,1)} copy(bf16[64,1,2,48,384]{4,3,2,1,0:T(8,128)(2,1)} %all-to-all-done.2) | data formatting | bytes 9437184 | tf_op jit(solution)/shard_map/all_to_all | solution.py:48
  174.0 36.9 %all-to-all-done.3 = bf16[64,1,2,48,384]{4,3,2,1,0:T(8,128)(2,1)} async-done(((bf16[64,1,2,48,384]{4,3,2,1,0:T(8,128)(2,1)}), bf16[64,1,2,48,384]{4,3,2,1,0:T(8,128)(2,1)}, u32[]{:S(2)}, u32[]{:S(2)}) %all-to-all-start.3) | async-done | bytes 4718624 | tf_op jit(solution)/shard_map/all_to_all | solution.py:48
  210.8 4.2 %copy.46 = bf16[64,1,2,48,384]{4,0,3,2,1:T(8,128)(2,1)S(1)} copy(bf16[64,1,2,48,384]{4,3,2,1,0:T(8,128)(2,1)} %all-to-all-done.3) | data formatting | bytes 9437184 | tf_op jit(solution)/shard_map/all_to_all | solution.py:48
  215.0 5.2 %multiply_convert_fusion = bf16[64,2,96,384]{3,0,2,1:T(8,128)(2,1)} fusion(f32[96,384]{1,0:T(8,128)S(1)} %copy-done.1, bf16[64,64,1,1]{1,0,3,2:T(8,128)(2,1)S(1)} %fusion.9, bf16[64,1,2,48,384]{4,0,3,2,1:T(8,128)(2,1)S(1)} %copy.46, bf16[64,1,2,48,384]{4,0,3,2,1:T(8,128)(2,1)S(1)} %copy-done), kind=kOutput, calls=%fused_computation.6 | convolution fusion | flops 632291328 | bytes 19030016 | tf_op jit(solution)/shard_map/ij,iabc->jabc/dot_general | solution.py:151
  220.2 12.9 %copy.48 = bf16[64,2,96,384]{3,2,1,0:T(8,128)(2,1)} copy(bf16[64,2,96,384]{3,0,2,1:T(8,128)(2,1)} %multiply_convert_fusion) | data formatting | bytes 18874368 | tf_op jit(solution)/shard_map/convert_element_type | solution.py:154
  233.1 117.3 %all_to_all.31 = bf16[64,2,96,384]{3,2,1,0:T(8,128)(2,1)S(1)} all-to-all(bf16[64,2,96,384]{3,2,1,0:T(8,128)(2,1)} %copy.48), channel_id=1, replica_groups=mesh['member'=64,'cell'=2] {'member'}, dimensions={0} | all-to-all | bytes 18874368 | tf_op jit(solution)/shard_map/all_to_all | solution.py:155
  350.4 11.5 %convolution_convert_fusion = bf16[12288,384]{1,0:T(8,128)(2,1)} fusion(bf16[12288,384]{1,0:T(8,128)(2,1)S(1)} %bitcast.82, f32[384]{0:T(512)S(1)} %fusion.40, s32[384]{0:T(512)S(1)} %iota_add_fusion, pred[384]{0:T(512)(128)(4,1)S(1)} %iota_compare_fusion.4), kind=kOutput, calls=%fused_computation.7 | convolution fusion | flops 3630514176 | bytes 18877824 | tf_op jit(solution)/shard_map/dot_general | solution.py:112
  (120 shorter events, 9.0 us)
Async XLA Ops:
  17.0 12.7 %copy-start.5 = (s32[2048]{0:T(1024)S(1)}, s32[2048]{0:T(1024)}, u32[]{:S(2)}) copy-start(s32[2048]{0:T(1024)} %param.9) | copy-start | bytes 24580
  50.4 26.6 %all-to-all-start.1 = ((f32[64,2048,1]{1,2,0:T(1,128)}), f32[64,2048,1]{1,2,0:T(1,128)S(1)}, u32[]{:S(2)}, u32[]{:S(2)}) async-start(f32[64,2048,1]{1,2,0:T(1,128)} %broadcast_in_dim.30), calls=%async_computation.1 | async-start | bytes 1048576 | tf_op jit(solution)/shard_map/all_to_all | solution.py:11
  71.7 11.1 %copy-start.2 = (f32[2048]{0:T(1024)S(1)}, f32[2048]{0:T(1024)}, u32[]{:S(2)}) copy-start(f32[2048]{0:T(1024)} %param.11) | copy-start | bytes 24580
  71.7 11.1 %copy-start.3 = (f32[2048]{0:T(1024)S(1)}, f32[2048]{0:T(1024)}, u32[]{:S(2)}) copy-start(f32[2048]{0:T(1024)} %param.12) | copy-start | bytes 24580
  71.7 11.1 %copy-start.4 = (s32[2048]{0:T(1024)S(1)}, s32[2048]{0:T(1024)}, u32[]{:S(2)}) copy-start(s32[2048]{0:T(1024)} %param.10) | copy-start | bytes 24580
  77.0 65.4 %all-to-all-start.2 = ((bf16[64,1,2,48,384]{4,3,2,1,0:T(8,128)(2,1)}), bf16[64,1,2,48,384]{4,3,2,1,0:T(8,128)(2,1)}, u32[]{:S(2)}, u32[]{:S(2)}) async-start(bf16[64,1,2,48,384]{4,3,2,1,0:T(8,128)(2,1)} %get-tuple-element.59), calls=%async_computation.2 | async-start | bytes 9437184 | tf_op jit(solution)/shard_map/all_to_all | solution.py:48
  142.5 68.3 %all-to-all-start.3 = ((bf16[64,1,2,48,384]{4,3,2,1,0:T(8,128)(2,1)}), bf16[64,1,2,48,384]{4,3,2,1,0:T(8,128)(2,1)}, u32[]{:S(2)}, u32[]{:S(2)}) async-start(bf16[64,1,2,48,384]{4,3,2,1,0:T(8,128)(2,1)} %get-tuple-element.60), calls=%async_computation.3 | async-start | bytes 9437184 | tf_op jit(solution)/shard_map/all_to_all | solution.py:48
  167.7 47.3 %copy-start.1 = (f32[96,384]{1,0:T(8,128)S(1)}, f32[96,384]{1,0:T(8,128)}, u32[]{:S(2)}) copy-start(f32[96,384]{1,0:T(8,128)} %param.13) | copy-start | bytes 442372
  210.8 4.2 %copy-start = (bf16[64,1,2,48,384]{4,0,3,2,1:T(8,128)(2,1)S(1)}, bf16[64,1,2,48,384]{4,0,3,2,1:T(8,128)(2,1)}, u32[]{:S(2)}) copy-start(bf16[64,1,2,48,384]{4,0,3,2,1:T(8,128)(2,1)} %copy.45) | copy-start | bytes 14155780
where the time goes:
time: 363 us; the launch traced here: 362 us
  blocking collectives  123 us (34%)
  waiting for transfers between devices  99.6 us (27%)
  local copies, waits for them, and re-layouts  57.7 us (16%)
  matrix products  50.2 us (14%)
  starting transfers between devices  26.7 us (7%)
    all_to_all x1, blocking collectives, on_device(): lax.all_to_all(changed, 'member', split_axis=0, concat_axis=1, tiled=True)  117 us
    all_to_all x2, waiting for transfers between devices, several_exchanges(): lax.all_to_all(piece, axis, split_axis=0, concat_axis=0, tiled=True)  94.3 us
    dot_general x2, matrix products, spectral_conversion_pass(): jnp.dot(predicted_layouts.reshape(-1, dimension_tuple[-1]), trigonometric...  28.4 us
    all_to_all x2, starting transfers between devices, several_exchanges(): lax.all_to_all(piece, axis, split_axis=0, concat_axis=0, tiled=True)  13.9 us
    convert_element_type x1, local copies, waits for them, and re-layouts, on_device(): (changed * harmonic_update_weight[None, None]).astype(jnp.bfloat16)  12.9 us
    all_to_all x1, starting transfers between devices, copy_for_each(): lax.all_to_all(jnp.broadcast_to(shard[None], (size, *shard.shape)), axis,...  12.8 us
    convert_element_type x1, local copies, waits for them, and re-layouts, spectral_conversion_pass(): return flat.astype(jnp.bfloat16).reshape(dimension_tuple)  12.7 us
    gather x1, local copies, waits for them, and re-layouts, on_device(): own_preds = boundary_innovation.reshape(-1)[probe_surface_harmonic]  11.8 us
  transfers between devices with their start and end apart: 3, of which 3 were waited for; matrix products, arithmetic and copies ran while one was open for 9% of the time, Pallas kernels for 0%

commit v1 on v0

v1 whole, which is shorter than its diff:
```python
import functools

import jax
import jax.numpy as jnp
import numpy as np
from jax import lax
from jax.experimental import pallas as pl
from jax.experimental.pallas import tpu as pltpu
from jax.sharding import PartitionSpec as P

NS_ITERS = 24
TILE = 16
LEAD = 2
STRIDE = 27
NT = (((1,), (1,)), ((), ()))


def dft_basis(length):
    rows = np.arange(length)[:, None]
    cols = np.arange(length)[None, :]
    half = length // 2
    frequency = np.where(cols <= half, cols, cols - half)
    phase = 2.0 * np.pi * (rows * frequency % length) / length
    table = np.where(cols <= half, np.cos(phase), np.sin(phase))
    edge = (cols == 0) | (cols == half)
    return (table * np.where(edge, np.sqrt(1.0 / length), np.sqrt(2.0 / length))).astype(np.float32)


def iota(shape, dim):
    return lax.broadcasted_iota(jnp.int32, shape, dim)


def eye(size):
    return (iota((size, size), 0) == iota((size, size), 1)).astype(jnp.float32)


def partner(me, k, members):
    offset = (k * STRIDE) % members
    core = (me % 2 + offset % 2) % 2
    x = ((me // 2) % 4 + (offset // 2) % 4) % 4
    z = ((me // 8) % 4 + (offset // 8) % 4) % 4
    y = (me // 32 + offset // 32) % 2
    return ((y * 4 + z) * 4 + x) * 2 + core


def thirds(a):
    first = a.astype(jnp.bfloat16)
    rest = a - first.astype(jnp.float32)
    second = rest.astype(jnp.bfloat16)
    return first, second, (rest - second.astype(jnp.float32)).astype(jnp.bfloat16)


def left_of(a):
    first, second, third = thirds(a)
    return jnp.concatenate([third, second, first, second, first, first], axis=1)


def product(a, b):
    first, second, third = thirds(b)
    right = jnp.concatenate([first, second, third, first, second, first], axis=0)
    return jnp.dot(left_of(a), right, preferred_element_type=jnp.float32)


def product_nt(a, b):
    first, second, third = thirds(b)
    right = jnp.concatenate([first, second, third, first, second, first], axis=1)
    return lax.dot_general(left_of(a), right, NT, preferred_element_type=jnp.float32)


def own_predictions(wall_ref, basis_t_ref, probe_ref, own_ref):
    planes, tile, modes = wall_ref.shape
    rows = planes * tile
    picked = iota((2 * planes, rows), 0)
    wanted = jnp.where(picked < planes, picked * tile + (tile - 1), (picked - planes) * tile + (tile - 2))
    pick = (iota((2 * planes, rows), 1) == wanted).astype(jnp.bfloat16)
    levels = jnp.dot(pick, wall_ref[...].reshape(rows, modes), preferred_element_type=jnp.float32)
    spectra_t = lax.dot_general(
        basis_t_ref[...], levels.astype(jnp.bfloat16), NT, preferred_element_type=jnp.float32
    ).astype(jnp.bfloat16)
    groups, width = own_ref.shape
    for g in range(groups):
        probe = probe_ref[:, g * width : (g + 1) * width]
        plane = ((probe >> 7) * 171) >> 9
        mode = probe - plane * modes
        row = iota((2 * planes, width), 0)
        sign = jnp.where(row == plane, 1.0, 0.0) - jnp.where(row == plane + planes, 1.0, 0.0)
        shear = jnp.dot(spectra_t, sign.astype(jnp.bfloat16), preferred_element_type=jnp.float32)
        taken = jnp.where(iota((modes, width), 0) == mode, shear, 0.0)
        own_ref[g : g + 1, :] = jnp.sum(taken, axis=0, keepdims=True)


def mixing_matrix(preds_ref, observed_ref, spread_ref, part_ref, block):
    members, groups, width = preds_ref.shape
    side = 128
    inside = (iota((side, side), 0) < members) & (iota((side, side), 1) < members)
    unit = eye(side) * inside.astype(jnp.float32)
    gram = (members - 1.0) * unit
    right = jnp.zeros((1, side), jnp.float32)
    empty = jnp.zeros((side - members, width), jnp.float32)
    for g in range(groups):
        lanes = slice(g * width, (g + 1) * width)
        preds = preds_ref[:, g, :]
        mean = jnp.sum(preds, axis=0, keepdims=True) * (1.0 / members)
        selector = jnp.where(part_ref[:, lanes] == block, 1.0, 0.0) / spread_ref[:, lanes]
        scaled = jnp.concatenate([(preds - mean) * selector, empty], axis=0)
        innovation = (observed_ref[:, lanes] - mean) * selector
        gram += product_nt(scaled, scaled)
        right += product_nt(jnp.broadcast_to(innovation, (16, width)), scaled)[:1]
    squares = jnp.sum(jnp.sum(gram * gram, axis=1, keepdims=True), axis=0, keepdims=True)
    norm = jnp.sqrt(squares)

    def newton_iter(count, carry):
        iterate, inv_root = carry
        step = 1.5 * unit - 0.5 * product(inv_root, iterate)
        return product(iterate, step), product(step, inv_root)

    _, inv_root = lax.fori_loop(0, NS_ITERS, newton_iter, (gram / norm, unit))
    root = inv_root / jnp.sqrt(norm)
    inv_gram = product(root, root)
    factors = jnp.sum(inv_gram * right, axis=1, keepdims=True)
    combined = factors + np.float32(np.sqrt(members - 1.0)) * root
    combined = jnp.where(inside, combined, 0.0)
    centred = combined - jnp.sum(combined, axis=0, keepdims=True) * (1.0 / members)
    return jnp.where(inside, (1.0 / members) + centred - unit, 0.0).astype(jnp.bfloat16)


def kernel(
    members,
    x_ref,
    basis_ref,
    basis_t_ref,
    probe_ref,
    part_ref,
    observed_ref,
    spread_ref,
    weight_ref,
    out_ref,
    wall,
    held,
    done,
    own,
    preds,
    spread_mix,
    spectra,
    wall_sem,
    give_sem,
    hold_sem,
    own_send,
    own_recv,
    preds_send,
    preds_recv,
    back_send,
    back_recv,
):
    chunks = held.shape[0]
    deep = held.shape[2]
    me = lax.axis_index("member")
    cell = lax.axis_index("cell")
    at_wall = cell == 1
    barrier = pltpu.get_barrier_semaphore()

    wall_copy = pltpu.make_async_copy(x_ref.at[0, :, pl.ds((chunks - 1) * TILE, TILE)], wall, wall_sem)
    wall_copy.start()

    @pl.loop(1, members)
    def _(k):
        pl.semaphore_signal(barrier, inc=1, device_id={"member": (me + k) % members})

    pl.semaphore_signal(barrier, inc=1, device_id={"cell": 1 - cell})
    pl.semaphore_wait(barrier, members)

    def give(c):
        rows = pl.ds(c * TILE, TILE)
        pltpu.make_async_copy(
            x_ref.at[0, pl.ds(me * deep, deep), rows], held.at[c, me], hold_sem.at[c]
        ).start()

        @pl.loop(1, members)
        def _(k):
            p = partner(me, k, members)
            pltpu.make_async_remote_copy(
                src_ref=x_ref.at[0, pl.ds(p * deep, deep), rows],
                dst_ref=held.at[c, me],
                send_sem=give_sem,
                recv_sem=hold_sem.at[c],
                device_id={"member": p},
            ).start()

    for c in range(LEAD):
        give(c)

    wall_copy.wait()
    to_sibling = pltpu.make_async_remote_copy(
        src_ref=own, dst_ref=own, send_sem=own_send, recv_sem=own_recv, device_id={"cell": 0}
    )

    @pl.when(at_wall)
    def _():
        own_predictions(wall, basis_t_ref, probe_ref, own)
        to_sibling.start()
        to_sibling.wait_send()

    @pl.when(jnp.logical_not(at_wall))
    def _():
        to_sibling.wait_recv()

    pltpu.make_async_copy(own, preds.at[me], preds_recv).start()

    @pl.loop(1, members)
    def _(k):
        pltpu.make_async_remote_copy(
            src_ref=own,
            dst_ref=preds.at[me],
            send_sem=preds_send,
            recv_sem=preds_recv,
            device_id={"member": partner(me, k, members)},
        ).start()

    @pl.loop(LEAD, chunks)
    def _(c):
        give(c)

    pltpu.make_async_copy(preds, preds, preds_recv).wait()
    mixing = mixing_matrix(preds, observed_ref, spread_ref, part_ref, me)

    wide = members * TILE
    high = 128
    across = (iota((high, wide), 1) // TILE == iota((high, wide), 0)).astype(jnp.bfloat16)

    @pl.loop(0, wide // high)
    def _(b):
        member = (iota((high, high), 0) + b * high) // TILE
        down = (member == iota((high, high), 1)).astype(jnp.bfloat16)
        part = lax.dot_general(down, mixing, NT, preferred_element_type=jnp.float32).astype(jnp.bfloat16)
        full = jnp.dot(part, across, preferred_element_type=jnp.float32)
        same = iota((high, wide), 0) % TILE == iota((high, wide), 1) % TILE
        spread_mix[pl.ds(pl.multiple_of(b * high, high), high), :] = jnp.where(same, full, 0.0).astype(jnp.bfloat16)

    step = 256
    some = step // TILE

    @pl.loop(0, chunks)
    def _(c):
        pltpu.make_async_copy(held.at[c], held.at[c], hold_sem.at[c]).wait()
        rows = pl.ds(pl.multiple_of(c * TILE, TILE), TILE)

        @pl.loop(0, deep)
        def _(p):
            @pl.loop(0, wide // step)
            def _(b):
                field = held[c, pl.ds(b * some, some), p].reshape(step, -1)
                spectra[pl.ds(pl.multiple_of(b * step, step), step), :] = jnp.dot(
                    field, basis_ref[...], preferred_element_type=jnp.float32
                ).astype(jnp.bfloat16)

            @pl.loop(0, wide // step)
            def _(b):
                changed = jnp.dot(
                    spread_mix[pl.ds(pl.multiple_of(b * step, step), step), :],
                    spectra[...],
                    preferred_element_type=jnp.float32,
                )
                changed = changed.reshape(some, TILE, -1) * weight_ref[rows, :][None]
                changed = changed.astype(jnp.bfloat16).reshape(step, -1)
                back = jnp.dot(changed, basis_t_ref[...], preferred_element_type=jnp.float32)
                done[c, pl.ds(b * some, some), p] = back.astype(jnp.bfloat16).reshape(some, TILE, -1)

        pltpu.make_async_copy(
            done.at[c, me], out_ref.at[0, pl.ds(me * deep, deep), rows], back_recv
        ).start()

        @pl.loop(1, members)
        def _(k):
            p = partner(me, k, members)
            pltpu.make_async_remote_copy(
                src_ref=done.at[c, p],
                dst_ref=out_ref.at[0, pl.ds(me * deep, deep), rows],
                send_sem=back_send,
                recv_sem=back_recv,
                device_id={"member": p},
            ).start()

    others = pl.ds(0, members - 1)
    pltpu.make_async_copy(preds.at[others], preds.at[others], preds_send).wait()
    pltpu.make_async_copy(held.at[:, others], held.at[:, others], give_sem).wait()
    pltpu.make_async_copy(held.at[:, others], held.at[:, others], back_send).wait()
    pltpu.make_async_copy(out_ref, out_ref, back_recv).wait()


def on_device(members, x, probe, part, observed, spread, weight):
    _, planes, levels, modes = x.shape
    sensors = probe.shape[0]
    chunks = levels // TILE
    deep = planes // members
    table = dft_basis(modes)
    basis = jnp.asarray(table, jnp.bfloat16)
    basis_t = jnp.asarray(table.T, jnp.bfloat16)
    vmem = pl.BlockSpec(memory_space=pltpu.VMEM)
    anywhere = pl.BlockSpec(memory_space=pl.ANY)
    dma = pltpu.SemaphoreType.DMA(())
    return pl.pallas_call(
        functools.partial(kernel, members),
        out_shape=jax.ShapeDtypeStruct(x.shape, x.dtype),
        in_specs=[anywhere] + [vmem] * 7,
        out_specs=anywhere,
        scratch_shapes=[
            pltpu.VMEM((planes, TILE, modes), jnp.bfloat16),
            pltpu.VMEM((chunks, members, deep, TILE, modes), jnp.bfloat16),
            pltpu.VMEM((chunks, members, deep, TILE, modes), jnp.bfloat16),
            pltpu.VMEM((8, sensors // 8), jnp.float32),
            pltpu.VMEM((members, 8, sensors // 8), jnp.float32),
            pltpu.VMEM((members * TILE, members * TILE), jnp.bfloat16),
            pltpu.VMEM((members * TILE, modes), jnp.bfloat16),
            dma,
            dma,
            pltpu.SemaphoreType.DMA((chunks,)),
            dma,
            dma,
            dma,
            dma,
            dma,
            dma,
        ],
        compiler_params=pltpu.CompilerParams(
            collective_id=0, has_side_effects=True, vmem_limit_bytes=48 << 20
        ),
    )(x, basis, basis_t, probe[None], part[None], observed[None], spread[None], weight)


def solution(mesh):
    return jax.shard_map(
        functools.partial(on_device, mesh.shape["member"]),
        mesh=mesh,
        in_specs=(P("member", None, "cell", None), P(), P(), P(), P(), P("cell", None)),
        out_specs=P("member", None, "cell", None),
        check_vma=False,
    )
```

time: 363 us -> 237 us (0.65)
  Pallas kernels: 0 us -> 222 us
  blocking collectives: 123 us -> 0 us
  waiting for transfers between devices: 99.6 us -> 0 us
  matrix products: 50.2 us -> 0 us
  local copies, waits for them, and re-layouts: 57.7 us -> 14 us
  starting transfers between devices: 26.7 us -> 0 us
    pallas_call x0 -> x1, Pallas kernels: none -> 222 us  [on_device(): pl.pallas_call(functools.partial(kernel, members), out_shape=jax.ShapeDty...]
    all_to_all x2 -> x0, blocking collectives: 123 us -> none  [the longest x1 117 us: on_device(): lax.all_to_all(changed, 'member', split_axis=0, concat_axis=1, tiled=True)]
    all_to_all x3 -> x0, waiting for transfers between devices: 99.6 us -> none  [the longest x2 94.3 us: several_exchanges(): lax.all_to_all(piece, axis, split_axis=0, concat_axis=0, tiled=True)]
    dot_general x80 -> x0, matrix products: 50.2 us -> none  [the longest x2 28.4 us: spectral_conversion_pass(): jnp.dot(predicted_layouts.reshape(-1, dimension_tuple[-1]), trigonometric...]
    all_to_all x3 -> x0, starting transfers between devices: 26.7 us -> none  [the longest x2 13.9 us: several_exchanges(): lax.all_to_all(piece, axis, split_axis=0, concat_axis=0, tiled=True)]
    convert_element_type x2 -> x0, local copies, waits for them, and re-layouts: 25.6 us -> none  [the longest x1 12.9 us: on_device(): (changed * harmonic_update_weight[None, None]).astype(jnp.bfloat16)]
    unnamed x13 -> x15, local copies, waits for them, and re-layouts: 0.1 us -> 14 us
    gather x1 -> x0, local copies, waits for them, and re-layouts: 11.8 us -> none  [on_device(): own_preds = boundary_innovation.reshape(-1)[probe_surface_harmonic]]
  transfers between devices with their start and end apart: 3 -> 0, of which waited for: 3 -> 0; matrix products, arithmetic and copies ran while one was open for 9% -> 0% of each run, Pallas kernels for 0% -> 0%
where the time goes in v1:
time: 237 us; the launch traced here: 236 us
  Pallas kernels  222 us (94%)
  local copies, waits for them, and re-layouts  14 us (6%)
    pallas_call x1, Pallas kernels, on_device(): pl.pallas_call(functools.partial(kernel, members), out_shape=jax.ShapeDty...  222 us
    unnamed x15, local copies, waits for them, and re-layouts  14 us

profile of v1, /device:TPU:1, one launch (start us, length us, event | category | flops | bytes accessed | tf_op | source)
XLA Modules:
  0.0 236.5 jit_solution(9429544575359829528)
XLA Ops:
  0.0 0.0 copy-start
  0.0 1.0 copy-done
  1.0 0.0 copy-start.1
  1.0 1.0 copy-done.1
  1.9 0.0 copy-start.2
  1.9 0.9 copy-done.2
  2.8 0.0 copy-start.3
  2.8 0.7 copy-done.3
  3.5 0.0 copy-start.4
  3.5 0.7 copy-done.4
  4.2 0.0 copy-start.5
  4.2 0.7 copy-done.5
  4.9 0.0 copy-start.6
  4.9 0.7 copy-done.6
  5.6 222.5 %shard_map.82 = bf16[1,128,96,384]{3,2,1,0:T(8,128)(2,1)} custom-call(bf16[1,128,96,384]{3,2,1,0:T(8,128)(2,1)} %x_ref.1, bf16[384,384]{1,0:T(8,128)(2,1)S(1)} %copy-done.1, bf16[384,384]{1,0:T(8,128)(2,1)S(1)} %copy-done, s32[1,2048]{1,0:T(1,128)S(1)} %bitcast.4, s32[1,2048]{1,0:T(1,128)S(1)} %bitcast.5, f32[1,2048]{1,0:T(1,128)S(1)} %bitcast.6, ...), custom_call_target="tpu_custom_call" | custom-call | tf_op jit(solution)/shard_map/pallas_call | solution.py:301
  228.1 8.4 %copy.10 = bf16[1,128,96,384]{3,2,1,0:T(8,128)(2,1)} copy(bf16[1,128,96,384]{3,2,1,0:T(8,128)(2,1)} %shard_map.82) | data formatting | bytes 18874368
Async XLA Ops:
  0.0 1.0 copy-start
  1.0 1.0 copy-start.1
  1.9 0.9 copy-start.2
  2.8 0.7 copy-start.3
  3.5 0.7 copy-start.4
  4.2 0.7 copy-start.5
  4.9 0.7 copy-start.6

commit v2 on v1

--- a/solution.py
+++ b/solution.py
@@ -9,9 +9,9 @@
 from jax.sharding import PartitionSpec as P
 
 NS_ITERS = 24
+STRIDE = 37
 TILE = 16
-LEAD = 2
-STRIDE = 27
+LEAD = 3
 NT = (((1,), (1,)), ((), ()))
 
 
@@ -34,13 +34,21 @@
     return (iota((size, size), 0) == iota((size, size), 1)).astype(jnp.float32)
 
 
-def partner(me, k, members):
-    offset = (k * STRIDE) % members
-    core = (me % 2 + offset % 2) % 2
-    x = ((me // 2) % 4 + (offset // 2) % 4) % 4
-    z = ((me // 8) % 4 + (offset // 8) % 4) % 4
+def visits(members):
+    return [(k * STRIDE) % members for k in range(1, members)]
+
+
+def partner(me, offset):
+    core = me % 2
+    way = 1 + 2 * core
+    x = ((me // 2) % 4 + way * ((offset // 2) % 4)) % 4
+    z = ((me // 8) % 4 + way * ((offset // 8) % 4)) % 4
     y = (me // 32 + offset // 32) % 2
-    return ((y * 4 + z) * 4 + x) * 2 + core
+    return ((y * 4 + z) * 4 + x) * 2 + (core + offset % 2) % 2
+
+
+def by_core(member, members):
+    return (member % 2) * (members // 2) + member // 2
 
 
 def thirds(a):
@@ -90,7 +98,8 @@
 
 
 def mixing_matrix(preds_ref, observed_ref, spread_ref, part_ref, block):
-    members, groups, width = preds_ref.shape
+    cores, chips, groups, width = preds_ref.shape
+    members = cores * chips
     side = 128
     inside = (iota((side, side), 0) < members) & (iota((side, side), 1) < members)
     unit = eye(side) * inside.astype(jnp.float32)
@@ -99,7 +108,7 @@
     empty = jnp.zeros((side - members, width), jnp.float32)
     for g in range(groups):
         lanes = slice(g * width, (g + 1) * width)
-        preds = preds_ref[:, g, :]
+        preds = preds_ref[:, :, g, :].reshape(members, width)
         mean = jnp.sum(preds, axis=0, keepdims=True) * (1.0 / members)
         selector = jnp.where(part_ref[:, lanes] == block, 1.0, 0.0) / spread_ref[:, lanes]
         scaled = jnp.concatenate([(preds - mean) * selector, empty], axis=0)
@@ -127,6 +136,14 @@
 def kernel(
     members,
     x_ref,
+    basis_hbm,
+    basis_t_hbm,
+    probe_hbm,
+    part_hbm,
+    observed_hbm,
+    spread_hbm,
+    weight_hbm,
+    out_ref,
     basis_ref,
     basis_t_ref,
     probe_ref,
@@ -134,7 +151,7 @@
     observed_ref,
     spread_ref,
     weight_ref,
-    out_ref,
+    small_sem,
     wall,
     held,
     done,
@@ -149,18 +166,36 @@
     own_recv,
     preds_send,
     preds_recv,
+    core_send,
+    core_recv,
     back_send,
     back_recv,
 ):
-    chunks = held.shape[0]
-    deep = held.shape[2]
+    pieces, levels = held.shape[0], weight_ref.shape[0]
+    deep = pieces * TILE // levels
     me = lax.axis_index("member")
     cell = lax.axis_index("cell")
     at_wall = cell == 1
     barrier = pltpu.get_barrier_semaphore()
 
-    wall_copy = pltpu.make_async_copy(x_ref.at[0, :, pl.ds((chunks - 1) * TILE, TILE)], wall, wall_sem)
+    wall_copy = pltpu.make_async_copy(x_ref.at[0, :, pl.ds(levels - TILE, TILE)], wall, wall_sem)
     wall_copy.start()
+    small = [
+        pltpu.make_async_copy(source, target, small_sem.at[i])
+        for i, (source, target) in enumerate(
+            (
+                (basis_t_hbm, basis_t_ref),
+                (probe_hbm, probe_ref),
+                (basis_hbm, basis_ref),
+                (part_hbm, part_ref),
+                (observed_hbm, observed_ref),
+                (spread_hbm, spread_ref),
+                (weight_hbm, weight_ref),
+            )
+        )
+    ]
+    for copy in small:
+        copy.start()
 
     @pl.loop(1, members)
     def _(k):
@@ -169,27 +204,27 @@
     pl.semaphore_signal(barrier, inc=1, device_id={"cell": 1 - cell})
     pl.semaphore_wait(barrier, members)
 
-    def give(c):
-        rows = pl.ds(c * TILE, TILE)
-        pltpu.make_async_copy(
-            x_ref.at[0, pl.ds(me * deep, deep), rows], held.at[c, me], hold_sem.at[c]
-        ).start()
-
-        @pl.loop(1, members)
-        def _(k):
-            p = partner(me, k, members)
+    def give(u):
+        c, p = u // deep, u % deep
+        rows = pl.ds(pl.multiple_of(c * TILE, TILE), TILE)
+        pltpu.make_async_copy(x_ref.at[0, me * deep + p, rows], held.at[u, me], hold_sem.at[u]).start()
+        for offset in visits(members):
+            owner = partner(me, offset)
             pltpu.make_async_remote_copy(
-                src_ref=x_ref.at[0, pl.ds(p * deep, deep), rows],
-                dst_ref=held.at[c, me],
+                src_ref=x_ref.at[0, owner * deep + p, rows],
+                dst_ref=held.at[u, me],
                 send_sem=give_sem,
-                recv_sem=hold_sem.at[c],
-                device_id={"member": p},
+                recv_sem=hold_sem.at[u],
+                device_id={"member": owner},
             ).start()
 
-    for c in range(LEAD):
-        give(c)
+    @pl.loop(0, LEAD)
+    def _(u):
+        give(u)
 
     wall_copy.wait()
+    small[0].wait()
+    small[1].wait()
     to_sibling = pltpu.make_async_remote_copy(
         src_ref=own, dst_ref=own, send_sem=own_send, recv_sem=own_recv, device_id={"cell": 0}
     )
@@ -204,33 +239,44 @@
     def _():
         to_sibling.wait_recv()
 
-    pltpu.make_async_copy(own, preds.at[me], preds_recv).start()
-
-    @pl.loop(1, members)
-    def _(k):
-        pltpu.make_async_remote_copy(
-            src_ref=own,
-            dst_ref=preds.at[me],
-            send_sem=preds_send,
-            recv_sem=preds_recv,
-            device_id={"member": partner(me, k, members)},
-        ).start()
-
-    @pl.loop(LEAD, chunks)
-    def _(c):
-        give(c)
-
-    pltpu.make_async_copy(preds, preds, preds_recv).wait()
+    core, chip, chips = me % 2, me // 2, members // 2
+    pltpu.make_async_copy(own, preds.at[core, chip], preds_recv).start()
+    for offset in visits(members):
+        if offset % 2 == 0:
+            pltpu.make_async_remote_copy(
+                src_ref=own,
+                dst_ref=preds.at[core, chip],
+                send_sem=preds_send,
+                recv_sem=preds_recv,
+                device_id={"member": partner(me, offset)},
+            ).start()
+
+    @pl.loop(LEAD, pieces)
+    def _(u):
+        give(u)
+
+    for copy in small[2:]:
+        copy.wait()
+    pltpu.make_async_copy(preds.at[core], preds.at[core], preds_recv).wait()
+    to_core = pltpu.make_async_remote_copy(
+        src_ref=preds.at[core],
+        dst_ref=preds.at[core],
+        send_sem=core_send,
+        recv_sem=core_recv,
+        device_id={"member": me + 1 - 2 * core},
+    )
+    to_core.start()
+    to_core.wait()
     mixing = mixing_matrix(preds, observed_ref, spread_ref, part_ref, me)
 
     wide = members * TILE
     high = 128
-    across = (iota((high, wide), 1) // TILE == iota((high, wide), 0)).astype(jnp.bfloat16)
+    across = (by_core(iota((high, wide), 1) // TILE, members) == iota((high, wide), 0)).astype(jnp.bfloat16)
 
     @pl.loop(0, wide // high)
     def _(b):
         member = (iota((high, high), 0) + b * high) // TILE
-        down = (member == iota((high, high), 1)).astype(jnp.bfloat16)
+        down = (by_core(member, members) == iota((high, high), 1)).astype(jnp.bfloat16)
         part = lax.dot_general(down, mixing, NT, preferred_element_type=jnp.float32).astype(jnp.bfloat16)
         full = jnp.dot(part, across, preferred_element_type=jnp.float32)
         same = iota((high, wide), 0) % TILE == iota((high, wide), 1) % TILE
@@ -239,81 +285,102 @@
     step = 256
     some = step // TILE
 
-    @pl.loop(0, chunks)
-    def _(c):
-        pltpu.make_async_copy(held.at[c], held.at[c], hold_sem.at[c]).wait()
+    @pl.loop(0, pieces)
+    def _(u):
+        pltpu.make_async_copy(held.at[u], held.at[u], hold_sem.at[u]).wait()
+        c, p = u // deep, u % deep
         rows = pl.ds(pl.multiple_of(c * TILE, TILE), TILE)
 
-        @pl.loop(0, deep)
-        def _(p):
-            @pl.loop(0, wide // step)
-            def _(b):
-                field = held[c, pl.ds(b * some, some), p].reshape(step, -1)
-                spectra[pl.ds(pl.multiple_of(b * step, step), step), :] = jnp.dot(
-                    field, basis_ref[...], preferred_element_type=jnp.float32
-                ).astype(jnp.bfloat16)
-
-            @pl.loop(0, wide // step)
-            def _(b):
-                changed = jnp.dot(
-                    spread_mix[pl.ds(pl.multiple_of(b * step, step), step), :],
-                    spectra[...],
-                    preferred_element_type=jnp.float32,
-                )
-                changed = changed.reshape(some, TILE, -1) * weight_ref[rows, :][None]
-                changed = changed.astype(jnp.bfloat16).reshape(step, -1)
-                back = jnp.dot(changed, basis_t_ref[...], preferred_element_type=jnp.float32)
-                done[c, pl.ds(b * some, some), p] = back.astype(jnp.bfloat16).reshape(some, TILE, -1)
-
-        pltpu.make_async_copy(
-            done.at[c, me], out_ref.at[0, pl.ds(me * deep, deep), rows], back_recv
-        ).start()
-
-        @pl.loop(1, members)
-        def _(k):
-            p = partner(me, k, members)
+        @pl.loop(0, wide // step)
+        def _(b):
+            field = held[u, pl.ds(b * some, some)].reshape(step, -1)
+            spectra[pl.ds(pl.multiple_of(b * step, step), step), :] = jnp.dot(
+                field, basis_ref[...], preferred_element_type=jnp.float32
+            ).astype(jnp.bfloat16)
+
+        @pl.loop(0, wide // step)
+        def _(b):
+            changed = jnp.dot(
+                spread_mix[pl.ds(pl.multiple_of(b * step, step), step), :],
+                spectra[...],
+                preferred_element_type=jnp.float32,
+            )
+            changed = changed.reshape(some, TILE, -1) * weight_ref[rows, :][None]
+            changed = changed.astype(jnp.bfloat16).reshape(step, -1)
+            back = jnp.dot(changed, basis_t_ref[...], preferred_element_type=jnp.float32)
+            done[u, pl.ds(b * some, some)] = back.astype(jnp.bfloat16).reshape(some, TILE, -1)
+
+        target = out_ref.at[0, me * deep + p, rows]
+        pltpu.make_async_copy(done.at[u, me], target, back_recv).start()
+        for offset in visits(members):
+            member = partner(me, offset)
             pltpu.make_async_remote_copy(
-                src_ref=done.at[c, p],
-                dst_ref=out_ref.at[0, pl.ds(me * deep, deep), rows],
+                src_ref=done.at[u, member],
+                dst_ref=target,
                 send_sem=back_send,
                 recv_sem=back_recv,
-                device_id={"member": p},
+                device_id={"member": member},
             ).start()
 
     others = pl.ds(0, members - 1)
-    pltpu.make_async_copy(preds.at[others], preds.at[others], preds_send).wait()
+    far = preds.at[0, pl.ds(0, chips - 1)]
+    pltpu.make_async_copy(far, far, preds_send).wait()
     pltpu.make_async_copy(held.at[:, others], held.at[:, others], give_sem).wait()
     pltpu.make_async_copy(held.at[:, others], held.at[:, others], back_send).wait()
     pltpu.make_async_copy(out_ref, out_ref, back_recv).wait()
 
 
+def copy_out(source, target, buffer, come, go):
+    parts = buffer.shape[0]
+    deep = buffer.shape[2]
+    reads, writes = [], []
+    for i in range(parts):
+        planes = pl.ds(i * deep, deep)
+        reads.append(pltpu.make_async_copy(source.at[:, planes], buffer.at[i], come.at[i]))
+        writes.append(pltpu.make_async_copy(buffer.at[i], target.at[:, planes], go.at[i]))
+        reads[-1].start()
+    for i in range(parts):
+        reads[i].wait()
+        writes[i].start()
+    for i in range(parts):
+        writes[i].wait()
+
+
 def on_device(members, x, probe, part, observed, spread, weight):
     _, planes, levels, modes = x.shape
     sensors = probe.shape[0]
-    chunks = levels // TILE
-    deep = planes // members
+    pieces = (levels // TILE) * (planes // members)
     table = dft_basis(modes)
     basis = jnp.asarray(table, jnp.bfloat16)
     basis_t = jnp.asarray(table.T, jnp.bfloat16)
-    vmem = pl.BlockSpec(memory_space=pltpu.VMEM)
-    anywhere = pl.BlockSpec(memory_space=pl.ANY)
+    hbm = pl.BlockSpec(memory_space=pltpu.HBM)
     dma = pltpu.SemaphoreType.DMA(())
-    return pl.pallas_call(
+    increments = pl.pallas_call(
         functools.partial(kernel, members),
         out_shape=jax.ShapeDtypeStruct(x.shape, x.dtype),
-        in_specs=[anywhere] + [vmem] * 7,
-        out_specs=anywhere,
+        in_specs=[hbm] * 8,
+        out_specs=hbm,
         scratch_shapes=[
+            pltpu.VMEM((modes, modes), jnp.bfloat16),
+            pltpu.VMEM((modes, modes), jnp.bfloat16),
+            pltpu.VMEM((1, sensors), jnp.int32),
+            pltpu.VMEM((1, sensors), jnp.int32),
+            pltpu.VMEM((1, sensors), jnp.float32),
+            pltpu.VMEM((1, sensors), jnp.float32),
+            pltpu.VMEM((levels, modes), jnp.float32),
+            pltpu.SemaphoreType.DMA((7,)),
             pltpu.VMEM((planes, TILE, modes), jnp.bfloat16),
-            pltpu.VMEM((chunks, members, deep, TILE, modes), jnp.bfloat16),
-            pltpu.VMEM((chunks, members, deep, TILE, modes), jnp.bfloat16),
+            pltpu.VMEM((pieces, members, TILE, modes), jnp.bfloat16),
+            pltpu.VMEM((pieces, members, TILE, modes), jnp.bfloat16),
             pltpu.VMEM((8, sensors // 8), jnp.float32),
-            pltpu.VMEM((members, 8, sensors // 8), jnp.float32),
+            pltpu.VMEM((2, members // 2, 8, sensors // 8), jnp.float32),
             pltpu.VMEM((members * TILE, members * TILE), jnp.bfloat16),
             pltpu.VMEM((members * TILE, modes), jnp.bfloat16),
             dma,
             dma,
-            pltpu.SemaphoreType.DMA((chunks,)),
+            pltpu.SemaphoreType.DMA((pieces,)),
+            dma,
+            dma,
             dma,
             dma,
             dma,
@@ -322,9 +389,22 @@
             dma,
         ],
         compiler_params=pltpu.CompilerParams(
-            collective_id=0, has_side_effects=True, vmem_limit_bytes=48 << 20
+            collective_id=0, has_side_effects=True, vmem_limit_bytes=60 << 20
         ),
     )(x, basis, basis_t, probe[None], part[None], observed[None], spread[None], weight)
+    parts = 8
+    return pl.pallas_call(
+        copy_out,
+        out_shape=jax.ShapeDtypeStruct(x.shape, x.dtype),
+        in_specs=[hbm],
+        out_specs=hbm,
+        scratch_shapes=[
+            pltpu.VMEM((parts, 1, planes // parts, levels, modes), x.dtype),
+            pltpu.SemaphoreType.DMA((parts,)),
+            pltpu.SemaphoreType.DMA((parts,)),
+        ],
+        compiler_params=pltpu.CompilerParams(vmem_limit_bytes=60 << 20),
+    )(increments)
 
 
 def solution(mesh):

time: 237 us -> 227 us (0.958)
  local copies, waits for them, and re-layouts: 14 us -> 0 us
  Pallas kernels: 222 us -> 226 us
    unnamed x15 -> x0, local copies, waits for them, and re-layouts: 14 us -> none
    pallas_call x0 -> x1, Pallas kernels: none -> 7.35 us  [on_device(): pl.pallas_call(copy_out, out_shape=jax.ShapeDtypeStruct(x.shape, x.dtype)...]
    pallas_call x1, Pallas kernels: 222 us -> 219 us  [on_device(): pl.pallas_call(functools.partial(kernel, members), out_shape=jax.ShapeDty...]
where the time goes in v2:
time: 227 us; the launch traced here: 226 us
  Pallas kernels  226 us (100%)
    pallas_call x1, Pallas kernels, on_device(): pl.pallas_call(functools.partial(kernel, members), out_shape=jax.ShapeDty...  219 us
    pallas_call x1, Pallas kernels, on_device(): pl.pallas_call(copy_out, out_shape=jax.ShapeDtypeStruct(x.shape, x.dtype)...  7.35 us

profile of v2, /device:TPU:1, one launch (start us, length us, event | category | flops | bytes accessed | tf_op | source)
XLA Modules:
  0.0 226.4 jit_solution(10196723429781860854)
XLA Ops:
  0.0 219.0 %shard_map.82.source = bf16[1,128,96,384]{3,2,1,0:T(8,128)(2,1)} custom-call(bf16[1,128,96,384]{3,2,1,0:T(8,128)(2,1)} %x_ref.1, bf16[384,384]{1,0:T(8,128)(2,1)} %constant.4.clone.basis_hbm, bf16[384,384]{1,0:T(8,128)(2,1)} %constant.5.clone.basis_t_hbm, s32[1,2048]{1,0:T(1,128)} %bitcast.4, s32[1,2048]{1,0:T(1,128)} %bitcast.5, f32[1,2048]{1,0:T(1,128)} %bitcast.6, ...), custom_call_target="tpu_custom_call" | custom-call | tf_op jit(solution)/shard_map/pallas_call | solution.py:358
  219.1 7.3 %shard_map.83 = bf16[1,128,96,384]{3,2,1,0:T(8,128)(2,1)} custom-call(bf16[1,128,96,384]{3,2,1,0:T(8,128)(2,1)} %shard_map.82.source), custom_call_target="tpu_custom_call" | custom-call | tf_op jit(solution)/shard_map/pallas_call | solution.py:396

commit v3 on v2

--- a/solution.py
+++ b/solution.py
@@ -330,20 +330,16 @@
     pltpu.make_async_copy(out_ref, out_ref, back_recv).wait()
 
 
-def copy_out(source, target, buffer, come, go):
-    parts = buffer.shape[0]
-    deep = buffer.shape[2]
-    reads, writes = [], []
+def copy_out(source, target, go):
+    parts = go.shape[0]
+    deep = source.shape[1] // parts
+    writes = []
     for i in range(parts):
         planes = pl.ds(i * deep, deep)
-        reads.append(pltpu.make_async_copy(source.at[:, planes], buffer.at[i], come.at[i]))
-        writes.append(pltpu.make_async_copy(buffer.at[i], target.at[:, planes], go.at[i]))
-        reads[-1].start()
-    for i in range(parts):
-        reads[i].wait()
-        writes[i].start()
-    for i in range(parts):
-        writes[i].wait()
+        writes.append(pltpu.make_async_copy(source.at[:, planes], target.at[:, planes], go.at[i]))
+        writes[-1].start()
+    for write in writes:
+        write.wait()
 
 
 def on_device(members, x, probe, part, observed, spread, weight):
@@ -353,13 +349,14 @@
     table = dft_basis(modes)
     basis = jnp.asarray(table, jnp.bfloat16)
     basis_t = jnp.asarray(table.T, jnp.bfloat16)
+    vmem = pl.BlockSpec(memory_space=pltpu.VMEM)
     hbm = pl.BlockSpec(memory_space=pltpu.HBM)
     dma = pltpu.SemaphoreType.DMA(())
     increments = pl.pallas_call(
         functools.partial(kernel, members),
         out_shape=jax.ShapeDtypeStruct(x.shape, x.dtype),
         in_specs=[hbm] * 8,
-        out_specs=hbm,
+        out_specs=vmem,
         scratch_shapes=[
             pltpu.VMEM((modes, modes), jnp.bfloat16),
             pltpu.VMEM((modes, modes), jnp.bfloat16),
@@ -389,21 +386,19 @@
             dma,
         ],
         compiler_params=pltpu.CompilerParams(
-            collective_id=0, has_side_effects=True, vmem_limit_bytes=60 << 20
+            collective_id=0, has_side_effects=True, vmem_limit_bytes=37748736
         ),
-    )(x, basis, basis_t, probe[None], part[None], observed[None], spread[None], weight)
+    )(x, *(pltpu.with_memory_space_constraint(a, pltpu.HBM) for a in (basis, basis_t, probe[None], part[None], observed[None], spread[None], weight)))
     parts = 8
     return pl.pallas_call(
         copy_out,
         out_shape=jax.ShapeDtypeStruct(x.shape, x.dtype),
-        in_specs=[hbm],
+        in_specs=[vmem],
         out_specs=hbm,
         scratch_shapes=[
-            pltpu.VMEM((parts, 1, planes // parts, levels, modes), x.dtype),
-            pltpu.SemaphoreType.DMA((parts,)),
             pltpu.SemaphoreType.DMA((parts,)),
         ],
-        compiler_params=pltpu.CompilerParams(vmem_limit_bytes=60 << 20),
+        compiler_params=pltpu.CompilerParams(vmem_limit_bytes=1 << 20),
     )(increments)
 
 

time: 227 us -> 223 us (0.982)
  Pallas kernels: 226 us -> 223 us
    pallas_call x1, Pallas kernels: 7.35 us -> 3.7 us  [on_device(): pl.pallas_call(copy_out, out_shape=jax.ShapeDtypeStruct(x.shape, x.dtype)...]
where the time goes in v3:
time: 223 us
  Pallas kernels  223 us (100%)
    pallas_call x1, Pallas kernels, on_device(): pl.pallas_call(functools.partial(kernel, members), out_shape=jax.ShapeDty...  219 us

profile of v3, /device:TPU:1, one launch (start us, length us, event | category | flops | bytes accessed | tf_op | source)
XLA Modules:
  0.0 222.7 jit_solution(3979848358349151295)
XLA Ops:
  0.0 218.9 %shard_map.82.source = bf16[1,128,96,384]{3,2,1,0:T(8,128)(2,1)S(1)} custom-call(bf16[1,128,96,384]{3,2,1,0:T(8,128)(2,1)} %x_ref.1, bf16[384,384]{1,0:T(8,128)(2,1)} %constant.4.clone.basis_hbm, bf16[384,384]{1,0:T(8,128)(2,1)} %constant.5.clone.basis_t_hbm, s32[1,2048]{1,0:T(1,128)} %bitcast.4, s32[1,2048]{1,0:T(1,128)} %bitcast.5, f32[1,2048]{1,0:T(1,128)} %bitcast.6, ...), custom_call_target="tpu_custom_call" | custom-call | tf_op jit(solution)/shard_map/pallas_call | solution.py:355
  219.0 3.7 %shard_map.83 = bf16[1,128,96,384]{3,2,1,0:T(8,128)(2,1)} custom-call(bf16[1,128,96,384]{3,2,1,0:T(8,128)(2,1)S(1)} %shard_map.82.source), custom_call_target="tpu_custom_call" | custom-call | tf_op jit(solution)/shard_map/pallas_call | solution.py:393

commit v4 on v3

--- a/solution.py
+++ b/solution.py
@@ -11,6 +11,7 @@
 NS_ITERS = 24
 STRIDE = 37
 TILE = 16
+LAST = 2
 LEAD = 3
 NT = (((1,), (1,)), ((), ()))
 
@@ -36,6 +37,11 @@
 
 def visits(members):
     return [(k * STRIDE) % members for k in range(1, members)]
+
+
+def hops(offset):
+    across = [0, 1, 2, 1]
+    return across[(offset // 2) % 4] + across[(offset // 8) % 4] + 2 * (offset // 32)
 
 
 def partner(me, offset):
@@ -312,15 +318,25 @@
 
         target = out_ref.at[0, me * deep + p, rows]
         pltpu.make_async_copy(done.at[u, me], target, back_recv).start()
-        for offset in visits(members):
-            member = partner(me, offset)
-            pltpu.make_async_remote_copy(
-                src_ref=done.at[u, member],
-                dst_ref=target,
-                send_sem=back_send,
-                recv_sem=back_recv,
-                device_id={"member": member},
-            ).start()
+
+        def give_back(order):
+            for offset in order:
+                member = partner(me, offset)
+                pltpu.make_async_remote_copy(
+                    src_ref=done.at[u, member],
+                    dst_ref=target,
+                    send_sem=back_send,
+                    recv_sem=back_recv,
+                    device_id={"member": member},
+                ).start()
+
+        @pl.when(u < pieces - LAST)
+        def _():
+            give_back(visits(members))
+
+        @pl.when(u >= pieces - LAST)
+        def _():
+            give_back(sorted(visits(members), key=lambda offset: -hops(offset)))
 
     others = pl.ds(0, members - 1)
     far = preds.at[0, pl.ds(0, chips - 1)]

time: 223 us -> 222 us (level)
  no operation moved by 1% of the time
where the time goes in v4:
time: 222 us
  Pallas kernels  222 us (100%)
    pallas_call x1, Pallas kernels, on_device(): pl.pallas_call(functools.partial(kernel, members), out_shape=jax.ShapeDty...  218 us

profile of v4, /device:TPU:1, one launch (start us, length us, event | category | flops | bytes accessed | tf_op | source)
XLA Modules:
  0.0 222.1 jit_solution(3765336613233741602)
XLA Ops:
  0.0 218.4 %shard_map.82.source = bf16[1,128,96,384]{3,2,1,0:T(8,128)(2,1)S(1)} custom-call(bf16[1,128,96,384]{3,2,1,0:T(8,128)(2,1)} %x_ref.1, bf16[384,384]{1,0:T(8,128)(2,1)} %constant.4.clone.basis_hbm, bf16[384,384]{1,0:T(8,128)(2,1)} %constant.5.clone.basis_t_hbm, s32[1,2048]{1,0:T(1,128)} %bitcast.4, s32[1,2048]{1,0:T(1,128)} %bitcast.5, f32[1,2048]{1,0:T(1,128)} %bitcast.6, ...), custom_call_target="tpu_custom_call" | custom-call | tf_op jit(solution)/shard_map/pallas_call | solution.py:371
  218.4 3.7 %shard_map.83 = bf16[1,128,96,384]{3,2,1,0:T(8,128)(2,1)} custom-call(bf16[1,128,96,384]{3,2,1,0:T(8,128)(2,1)S(1)} %shard_map.82.source), custom_call_target="tpu_custom_call" | custom-call | tf_op jit(solution)/shard_map/pallas_call | solution.py:409
